TPU v7x, 32 devices: a whole 2x2x4 slice. The times are simulated.
32 devices in a mesh: parts: 2 (over y), pix: 4 (over z), par: 4 (over x, core).
Axes of the slice: x: 2, y: 2, z: 4, core: 2. Of those that a mesh axis runs over, the one named last changes fastest.
Arguments:
- green_matrix: bfloat16 [4608, 16384], P('pix', 'par'), may hold values from -0.046875 to 0.046875
- observed: bfloat16 [64, 4608], P('parts', 'pix'), parts along dimension 0, may hold values from -1000 to 1000
Outputs:
- solution: float32 [64, 16384], P('parts', 'par'), parts along dimension 0
- residual: float32 [64, 4608], P('parts', 'pix'), parts along dimension 0
There are 2 independent parts, one for each index of `parts`. A program takes and returns all parts, laid end to end along the dimension named above; an argument that names none is the same for every part. Nothing has to cross between parts.
All inputs are finite; a program needn't handle non-finite values.
Results may differ from a plain program's by a relative error of at most 0.0038.
Values may be sent and summed in bfloat16 or wider, within the bound.
A program may use at most 64 MiB of HBM per device.

v0:
```python
import jax
import jax.numpy as jnp
from jax import lax
from jax.sharding import PartitionSpec as P

GRID = 128
ITERS = 5


def padded_2(block, sides, width):
    for axis, dim in sides:
        count = lax.axis_size(axis)
        forward = [(i, i + 1) for i in range(count - 1)]
        backward = [(target, source) for source, target in forward]
        low = lax.ppermute(
            lax.slice_in_dim(block, block.shape[dim] - width, None, axis=dim), axis, forward
        )
        high = lax.ppermute(lax.slice_in_dim(block, 0, width, axis=dim), axis, backward)
        block = jnp.concatenate([low, block, high], axis=dim)
    return block


def smooth(values):
    set_count = values.shape[0]
    grid_rows = values.shape[1] // GRID
    tiles = values.reshape(set_count, grid_rows, GRID)
    padded = padded_2(tiles, (("par", 1),), 1)
    padded = jnp.pad(padded, ((0, 0), (0, 0), (1, 1)))
    beside_all = (
        padded[:, 2:, 1:-1] + padded[:, :-2, 1:-1] + padded[:, 1:-1, 2:] + padded[:, 1:-1, :-2]
    )
    return (0.25 * (4.0 * tiles - beside_all)).reshape(set_count, grid_rows * GRID)


def forward(rounded, green_matrix):
    partial_value = lax.dot_general(
        rounded, green_matrix, (((1,), (1,)), ((), ())), preferred_element_type=jnp.float32
    )
    return lax.psum(partial_value, "par")


def curvatures(image, smoothed):
    local_image = jnp.sum(image * image, axis=1)
    local_smooth = jnp.sum(smoothed * smoothed, axis=1)
    image_sq = lax.psum(local_image, "pix")
    smooth_sq = lax.psum(local_smooth, "par")
    return image_sq + smooth_sq


def backward_sum(rounded, green_matrix):
    return lax.psum(jnp.dot(rounded, green_matrix, preferred_element_type=jnp.float32), "pix")


def column_squares(gradient):
    return lax.psum(jnp.sum(gradient * gradient, axis=1), "par")


def on_device(green_matrix, observed):
    set_count = observed.shape[0]
    tile_cells = green_matrix.shape[1]
    residual = observed.astype(jnp.float32)
    gradient = backward_sum(observed, green_matrix)
    grad_sq = column_squares(gradient)
    direction = gradient
    solution = jnp.zeros((set_count, tile_cells), jnp.float32)
    smooth_res = jnp.zeros((set_count, tile_cells), jnp.float32)
    for sweep in range(ITERS):
        rounded = direction.astype(jnp.bfloat16)
        image = forward(rounded, green_matrix)
        smoothed = smooth(lax.optimization_barrier(rounded).astype(jnp.float32))
        step_len = (grad_sq / curvatures(image, smoothed))[:, None]
        solution = solution + step_len * direction
        residual = residual - step_len * image
        smooth_res = smooth_res - step_len * smoothed
        if sweep + 1 < ITERS:
            gradient = backward_sum(residual.astype(jnp.bfloat16), green_matrix) + smooth(
                smooth_res
            )
            fresh_sq = column_squares(gradient)
            direction = gradient + (fresh_sq / grad_sq)[:, None] * direction
            grad_sq = fresh_sq
    return (solution, residual)


def solution(mesh):
    return jax.shard_map(
        on_device,
        mesh=mesh,
        in_specs=(P("pix", "par"), P("parts", "pix")),
        out_specs=(P("parts", "par"), P("parts", "pix")),
        check_vma=False,
    )
```

profile of v0, /device:TPU:0, one launch (start us, length us, event | category | flops | bytes accessed | tf_op | source)
XLA Modules:
  0.0 557.3 jit_solution(6629463593647099205)
XLA Ops:
  7.2 6.3 %fusion.53 = f32[32,4096]{1,0:T(8,128)} fusion(bf16[32,1152]{1,0:T(8,128)(2,1)} %param.3, bf16[1152,4096]{1,0:T(8,128)(2,1)} %param.2), kind=kOutput, calls=%fused_computation.150 | convolution fusion | flops 301989888 | bytes 10035200 | tf_op jit(solution)/shard_map/dot_general | solution.py:51
  13.5 41.3 %all-reduce.21.cloned.1.call-done = f32[32,4096]{1,0:T(8,128)} async-done(((f32[32,4096]{1,0:T(8,128)}), f32[32,4096]{1,0:T(8,128)}) %all-reduce.21.cloned.1.call-update) | async-done | bytes 524304 | tf_op jit(solution)/shard_map/psum | solution.py:51
  59.0 7.2 %fusion.54 = f32[32,1152]{1,0:T(8,128)} fusion(bf16[32,4096]{1,0:T(8,128)(2,1)S(1)} %get-tuple-element.45, bf16[1152,4096]{1,0:T(8,128)(2,1)} %param.2), kind=kOutput, calls=%fused_computation.151 | convolution fusion | flops 301989888 | bytes 9846784 | tf_op jit(solution)/shard_map/dot_general | solution.py:36
  67.5 8.5 %all-reduce.9 = (f32[32]{0:T(128)S(1)}, f32[32]{0:T(128)S(1)}) all-reduce(f32[32]{0:T(128)S(1)} %get-tuple-element.44, f32[32]{0:T(128)S(1)} %get-tuple-element.24), channel_id=1, replica_groups=mesh['parts'=2,'pix'=4,'par'=4] {'par'}, use_global_device_ids=true, to_apply=%region_2.0 | all-reduce | flops 64 | bytes 512 | tf_op jit(solution)/shard_map/psum | solution.py:55
  75.9 24.4 %all-reduce.23.cloned.1.call-done = f32[32,1152]{1,0:T(8,128)} async-done(((f32[32,1152]{1,0:T(8,128)}), f32[32,1152]{1,0:T(8,128)}) %all-reduce.23.cloned.1.call-update) | async-done | bytes 147472 | tf_op jit(solution)/shard_map/psum | solution.py:39
  101.3 11.7 %psum.178 = f32[32]{0:T(128)S(1)} all-reduce(f32[32]{0:T(128)S(1)} %multiply_reduce_fusion.13), channel_id=1, replica_groups=mesh['parts'=2,'pix'=4,'par'=4] {'pix'}, use_global_device_ids=true, to_apply=%region_5.6 | all-reduce | flops 32 | bytes 256 | tf_op jit(solution)/shard_map/psum | solution.py:45
  113.0 6.4 %fusion.28 = f32[32,4096]{1,0:T(8,128)} fusion(bf16[1152,4096]{1,0:T(8,128)(2,1)} %param.2, f32[32,1152]{1,0:T(8,128)} %all-reduce.23.cloned.1.call-done, bf16[32,1152]{1,0:T(8,128)(2,1)S(1)} %copy-done.9, f32[32]{0:T(128)S(1)} %get-tuple-element.23), kind=kOutput, calls=%fused_computation.121 | convolution fusion | flops 302137344 | bytes 10182784 | tf_op jit(solution)/shard_map/dot_general | solution.py:51
  122.2 3.3 collective-permute-done.2
  126.5 29.6 %all-reduce.25.cloned.1.call-done = f32[32,4096]{1,0:T(8,128)} async-done(((f32[32,4096]{1,0:T(8,128)}), f32[32,4096]{1,0:T(8,128)}) %all-reduce.25.cloned.1.call-update) | async-done | bytes 524304 | tf_op jit(solution)/shard_map/psum | solution.py:51
  156.1 1.5 multiply_reduce_fusion.6
  157.6 5.7 %psum.181 = f32[32]{0:T(128)S(1)} all-reduce(f32[32]{0:T(128)S(1)} %multiply_reduce_fusion.6), channel_id=1, replica_groups=mesh['parts'=2,'pix'=4,'par'=4] {'par'}, use_global_device_ids=true, to_apply=%region_10.11 | all-reduce | flops 32 | bytes 256 | tf_op jit(solution)/shard_map/psum | solution.py:55
  163.8 1.8 collective-permute-start.5
  166.9 7.2 %fusion.55 = f32[32,1152]{1,0:T(8,128)} fusion(bf16[32,4096]{1,0:T(8,128)(2,1)S(1)} %get-tuple-element.20, bf16[1152,4096]{1,0:T(8,128)(2,1)} %param.2), kind=kOutput, calls=%fused_computation.152 | convolution fusion | flops 301989888 | bytes 9846784 | tf_op jit(solution)/shard_map/dot_general | solution.py:36
  175.4 8.4 %psum.184 = f32[32]{0:T(128)S(1)} all-reduce(f32[32]{0:T(128)S(1)} %get-tuple-element.18), channel_id=1, replica_groups=mesh['parts'=2,'pix'=4,'par'=4] {'par'}, use_global_device_ids=true, to_apply=%region_15.16 | all-reduce | flops 32 | bytes 256 | tf_op jit(solution)/shard_map/psum | solution.py:46
  183.8 24.2 %all-reduce.27.cloned.1.call-done = f32[32,1152]{1,0:T(8,128)} async-done(((f32[32,1152]{1,0:T(8,128)}), f32[32,1152]{1,0:T(8,128)}) %all-reduce.27.cloned.1.call-update) | async-done | bytes 147472 | tf_op jit(solution)/shard_map/psum | solution.py:39
  209.0 11.7 %psum.183 = f32[32]{0:T(128)S(1)} all-reduce(f32[32]{0:T(128)S(1)} %multiply_reduce_fusion.12), channel_id=1, replica_groups=mesh['parts'=2,'pix'=4,'par'=4] {'pix'}, use_global_device_ids=true, to_apply=%region_13.14 | all-reduce | flops 32 | bytes 256 | tf_op jit(solution)/shard_map/psum | solution.py:45
  221.7 6.2 %fusion.34 = f32[32,4096]{1,0:T(8,128)} fusion(bf16[1152,4096]{1,0:T(8,128)(2,1)} %param.2, f32[32,1152]{1,0:T(8,128)S(1)} %multiply_subtract_fusion.7), kind=kOutput, calls=%fused_computation.126 | convolution fusion | flops 302026752 | bytes 10108928 | tf_op jit(solution)/shard_map/dot_general | solution.py:51
  230.8 3.3 collective-permute-done.6
  235.0 29.6 %all-reduce.29.cloned.1.call-done = f32[32,4096]{1,0:T(8,128)} async-done(((f32[32,4096]{1,0:T(8,128)}), f32[32,4096]{1,0:T(8,128)}) %all-reduce.29.cloned.1.call-update) | async-done | bytes 524304 | tf_op jit(solution)/shard_map/psum | solution.py:51
  264.6 1.5 multiply_reduce_fusion.4
  266.1 5.7 %psum.186 = f32[32]{0:T(128)S(1)} all-reduce(f32[32]{0:T(128)S(1)} %multiply_reduce_fusion.4), channel_id=1, replica_groups=mesh['parts'=2,'pix'=4,'par'=4] {'par'}, use_global_device_ids=true, to_apply=%region_18.19 | all-reduce | flops 32 | bytes 256 | tf_op jit(solution)/shard_map/psum | solution.py:55
  272.4 1.8 collective-permute-start.9
  275.4 7.2 %fusion.56 = f32[32,1152]{1,0:T(8,128)} fusion(bf16[32,4096]{1,0:T(8,128)(2,1)S(1)} %get-tuple-element.14, bf16[1152,4096]{1,0:T(8,128)(2,1)} %param.2), kind=kOutput, calls=%fused_computation.153 | convolution fusion | flops 301989888 | bytes 9846784 | tf_op jit(solution)/shard_map/dot_general | solution.py:36
  283.9 8.3 %psum.189 = f32[32]{0:T(128)S(1)} all-reduce(f32[32]{0:T(128)S(1)} %get-tuple-element.12), channel_id=1, replica_groups=mesh['parts'=2,'pix'=4,'par'=4] {'par'}, use_global_device_ids=true, to_apply=%region_23.24 | all-reduce | flops 32 | bytes 256 | tf_op jit(solution)/shard_map/psum | solution.py:46
  292.1 24.4 %all-reduce.31.cloned.1.call-done = f32[32,1152]{1,0:T(8,128)} async-done(((f32[32,1152]{1,0:T(8,128)}), f32[32,1152]{1,0:T(8,128)}) %all-reduce.31.cloned.1.call-update) | async-done | bytes 147472 | tf_op jit(solution)/shard_map/psum | solution.py:39
  317.5 11.7 %psum.188 = f32[32]{0:T(128)S(1)} all-reduce(f32[32]{0:T(128)S(1)} %multiply_reduce_fusion.11), channel_id=1, replica_groups=mesh['parts'=2,'pix'=4,'par'=4] {'pix'}, use_global_device_ids=true, to_apply=%region_21.22 | all-reduce | flops 32 | bytes 256 | tf_op jit(solution)/shard_map/psum | solution.py:45
  329.2 6.4 %fusion.32 = f32[32,4096]{1,0:T(8,128)} fusion(bf16[1152,4096]{1,0:T(8,128)(2,1)} %param.2, f32[32,1152]{1,0:T(8,128)S(1)} %multiply_subtract_fusion.7, f32[32,1152]{1,0:T(8,128)} %all-reduce.31.cloned.1.call-done, f32[32]{0:T(128)S(1)} %get-tuple-element.11), kind=kOutput, calls=%fused_computation.124 | convolution fusion | flops 302100480 | bytes 10256512 | tf_op jit(solution)/shard_map/dot_general | solution.py:51
  338.5 3.3 collective-permute-done.10
  342.7 29.6 %all-reduce.33.cloned.1.call-done = f32[32,4096]{1,0:T(8,128)} async-done(((f32[32,4096]{1,0:T(8,128)}), f32[32,4096]{1,0:T(8,128)}) %all-reduce.33.cloned.1.call-update) | async-done | bytes 524304 | tf_op jit(solution)/shard_map/psum | solution.py:51
  372.3 1.5 multiply_reduce_fusion.2
  373.7 5.7 %psum.191 = f32[32]{0:T(128)S(1)} all-reduce(f32[32]{0:T(128)S(1)} %multiply_reduce_fusion.2), channel_id=1, replica_groups=mesh['parts'=2,'pix'=4,'par'=4] {'par'}, use_global_device_ids=true, to_apply=%region_26.27 | all-reduce | flops 32 | bytes 256 | tf_op jit(solution)/shard_map/psum | solution.py:55
  381.0 1.8 collective-permute-start.13
  382.8 1.5 collective-permute-start.12
  384.3 7.2 %fusion.57 = f32[32,1152]{1,0:T(8,128)} fusion(bf16[32,4096]{1,0:T(8,128)(2,1)S(1)} %get-tuple-element.8, bf16[1152,4096]{1,0:T(8,128)(2,1)} %param.2), kind=kOutput, calls=%fused_computation.154 | convolution fusion | flops 301989888 | bytes 9846784 | tf_op jit(solution)/shard_map/dot_general | solution.py:36
  393.4 8.3 %psum.194 = f32[32]{0:T(128)S(1)} all-reduce(f32[32]{0:T(128)S(1)} %get-tuple-element.6), channel_id=1, replica_groups=mesh['parts'=2,'pix'=4,'par'=4] {'par'}, use_global_device_ids=true, to_apply=%region_31.32 | all-reduce | flops 32 | bytes 256 | tf_op jit(solution)/shard_map/psum | solution.py:46
  401.7 23.6 %all-reduce.35.cloned.1.call-done = f32[32,1152]{1,0:T(8,128)} async-done(((f32[32,1152]{1,0:T(8,128)}), f32[32,1152]{1,0:T(8,128)}) %all-reduce.35.cloned.1.call-update) | async-done | bytes 147472 | tf_op jit(solution)/shard_map/psum | solution.py:39
  426.4 11.7 %psum.193 = f32[32]{0:T(128)S(1)} all-reduce(f32[32]{0:T(128)S(1)} %multiply_reduce_fusion.10), channel_id=1, replica_groups=mesh['parts'=2,'pix'=4,'par'=4] {'pix'}, use_global_device_ids=true, to_apply=%region_29.30 | all-reduce | flops 32 | bytes 256 | tf_op jit(solution)/shard_map/psum | solution.py:45
  439.8 6.3 %fusion.30 = f32[32,4096]{1,0:T(8,128)} fusion(bf16[1152,4096]{1,0:T(8,128)(2,1)} %param.2, f32[32,1152]{1,0:T(8,128)S(1)} %multiply_subtract_fusion.5), kind=kOutput, calls=%fused_computation.122 | convolution fusion | flops 302026752 | bytes 10108928 | tf_op jit(solution)/shard_map/dot_general | solution.py:51
  448.9 3.3 collective-permute-done.14
  453.1 29.6 %all-reduce.37.cloned.1.call-done = f32[32,4096]{1,0:T(8,128)} async-done(((f32[32,4096]{1,0:T(8,128)}), f32[32,4096]{1,0:T(8,128)}) %all-reduce.37.cloned.1.call-update) | async-done | bytes 524304 | tf_op jit(solution)/shard_map/psum | solution.py:51
  482.7 1.5 multiply_reduce_fusion
  484.2 5.7 %psum.196 = f32[32]{0:T(128)S(1)} all-reduce(f32[32]{0:T(128)S(1)} %multiply_reduce_fusion), channel_id=1, replica_groups=mesh['parts'=2,'pix'=4,'par'=4] {'par'}, use_global_device_ids=true, to_apply=%region_34.35 | all-reduce | flops 32 | bytes 256 | tf_op jit(solution)/shard_map/psum | solution.py:55
  490.5 1.8 collective-permute-start.17
  493.5 7.2 %fusion.58 = f32[32,1152]{1,0:T(8,128)} fusion(bf16[32,4096]{1,0:T(8,128)(2,1)S(1)} %fusion.26, bf16[1152,4096]{1,0:T(8,128)(2,1)} %param.2), kind=kOutput, calls=%fused_computation.155 | convolution fusion | flops 301989888 | bytes 9846784 | tf_op jit(solution)/shard_map/dot_general | solution.py:36
  501.9 8.3 %psum.199 = f32[32]{0:T(128)S(1)} all-reduce(f32[32]{0:T(128)S(1)} %fusion.4), channel_id=1, replica_groups=mesh['parts'=2,'pix'=4,'par'=4] {'par'}, use_global_device_ids=true, to_apply=%region_39.40 | all-reduce | flops 32 | bytes 256 | tf_op jit(solution)/shard_map/psum | solution.py:46
  510.2 24.4 %all-reduce.39.cloned.1.call-done = f32[32,1152]{1,0:T(8,128)} async-done(((f32[32,1152]{1,0:T(8,128)}), f32[32,1152]{1,0:T(8,128)}) %all-reduce.39.cloned.1.call-update) | async-done | bytes 147472 | tf_op jit(solution)/shard_map/psum | solution.py:39
  535.6 11.7 %psum.198 = f32[32]{0:T(128)S(1)} all-reduce(f32[32]{0:T(128)S(1)} %multiply_reduce_fusion.9), channel_id=1, replica_groups=mesh['parts'=2,'pix'=4,'par'=4] {'pix'}, use_global_device_ids=true, to_apply=%region_37.38 | all-reduce | flops 32 | bytes 256 | tf_op jit(solution)/shard_map/psum | solution.py:45
  547.4 2.4 multiply_add_fusion
  (132 shorter events, 41.2 us)
Async XLA Ops:
  7.2 47.7 %all-reduce.21.cloned.1.call-start = ((), (), s32[]{:S(2)}) async-start(), calls=%async_computation | async-start | bytes 1048576 | tf_op jit(solution)/shard_map/psum | solution.py:51
  13.5 86.8 %all-reduce.23.cloned.1.call-start = ((), (), s32[]{:S(2)}) async-start(), calls=%async_computation.1 | async-start | bytes 294912 | tf_op jit(solution)/shard_map/psum | solution.py:39
  56.4 9.9 %collective-permute-start.1 = (f32[32,1,128]{2,1,0:T(1,128)S(1)}, f32[32,1,128]{2,1,0:T(1,128)S(1)}, u32[]{:S(2)}, u32[]{:S(2)}) collective-permute-start(f32[32,1,128]{2,1,0:T(1,128)S(1)} %get-tuple-element.42), channel_id=1, source_target_pairs={{0,1},{1,2},{2,3},{4,5},{5,6},{6,7},{8,9},{9,10},{10,11},{12,13},{... | collective-permute-start | bytes 49160 | tf_op jit(solution)/shard_map/ppermute | solution.py:15
  57.7 8.6 %collective-permute-start = (f32[32,1,128]{2,1,0:T(1,128)S(1)}, f32[32,1,128]{2,1,0:T(1,128)S(1)}, u32[]{:S(2)}, u32[]{:S(2)}) collective-permute-start(f32[32,1,128]{2,1,0:T(1,128)S(1)} %get-tuple-element.43), channel_id=1, source_target_pairs={{1,0},{2,1},{3,2},{5,4},{6,5},{7,6},{9,8},{10,9},{11,10},{13,12},{... | collective-permute-start | bytes 49160 | tf_op jit(solution)/shard_map/ppermute | solution.py:18
  66.3 89.8 %all-reduce.25.cloned.1.call-start = ((), (), s32[]{:S(2)}) async-start(), calls=%async_computation.2 | async-start | bytes 1048576 | tf_op jit(solution)/shard_map/psum | solution.py:51
  66.9 46.2 %copy-start.9 = (bf16[32,1152]{1,0:T(8,128)(2,1)S(1)}, bf16[32,1152]{1,0:T(8,128)(2,1)}, u32[]{:S(2)}) copy-start(bf16[32,1152]{1,0:T(8,128)(2,1)} %param.3) | copy-start | bytes 221188
  119.4 88.6 %all-reduce.27.cloned.1.call-start = ((), (), s32[]{:S(2)}) async-start(), calls=%async_computation.3 | async-start | bytes 294912 | tf_op jit(solution)/shard_map/psum | solution.py:39
  119.6 2.6 collective-permute-start.3
  120.9 4.6 collective-permute-start.2
  126.1 37.2 %copy-start = (f32[32,4096]{1,0:T(8,128)S(1)}, f32[32,4096]{1,0:T(8,128)}, u32[]{:S(2)}) copy-start(f32[32,4096]{1,0:T(8,128)} %all-reduce.21.cloned.1.call-done) | copy-start | bytes 1572868
  156.1 7.2 %copy-start.5 = (f32[32,4096]{1,0:T(8,128)S(1)}, f32[32,4096]{1,0:T(8,128)}, u32[]{:S(2)}) copy-start(f32[32,4096]{1,0:T(8,128)} %all-reduce.25.cloned.1.call-done) | copy-start | bytes 1572868
  163.8 10.4 %collective-permute-start.5 = (f32[32,1,128]{2,1,0:T(1,128)S(1)}, f32[32,1,128]{2,1,0:T(1,128)S(1)}, u32[]{:S(2)}, u32[]{:S(2)}) collective-permute-start(f32[32,1,128]{2,1,0:T(1,128)S(1)} %get-tuple-element.38), channel_id=1, source_target_pairs={{0,1},{1,2},{2,3},{4,5},{5,6},{6,7},{8,9},{9,10},{10,11},{12,13},{... | collective-permute-start | bytes 49160 | tf_op jit(solution)/shard_map/ppermute | solution.py:15
  165.6 8.6 %collective-permute-start.4 = (f32[32,1,128]{2,1,0:T(1,128)S(1)}, f32[32,1,128]{2,1,0:T(1,128)S(1)}, u32[]{:S(2)}, u32[]{:S(2)}) collective-permute-start(f32[32,1,128]{2,1,0:T(1,128)S(1)} %get-tuple-element.39), channel_id=1, source_target_pairs={{1,0},{2,1},{3,2},{5,4},{6,5},{7,6},{9,8},{10,9},{11,10},{13,12},{... | collective-permute-start | bytes 49160 | tf_op jit(solution)/shard_map/ppermute | solution.py:18
  174.2 90.4 %all-reduce.29.cloned.1.call-start = ((), (), s32[]{:S(2)}) async-start(), calls=%async_computation.4 | async-start | bytes 1048576 | tf_op jit(solution)/shard_map/psum | solution.py:51
  174.8 45.9 %copy-start.6 = (f32[32,1152]{1,0:T(8,128)S(1)}, f32[32,1152]{1,0:T(8,128)}, u32[]{:S(2)}) copy-start(f32[32,1152]{1,0:T(8,128)} %all-reduce.23.cloned.1.call-done) | copy-start | bytes 442372
  228.0 88.5 %all-reduce.31.cloned.1.call-start = ((), (), s32[]{:S(2)}) async-start(), calls=%async_computation.5 | async-start | bytes 294912 | tf_op jit(solution)/shard_map/psum | solution.py:39
  228.2 2.6 collective-permute-start.7
  229.5 4.6 collective-permute-start.6
  264.6 7.2 %copy-start.4 = (f32[32,4096]{1,0:T(8,128)S(1)}, f32[32,4096]{1,0:T(8,128)}, u32[]{:S(2)}) copy-start(f32[32,4096]{1,0:T(8,128)} %all-reduce.29.cloned.1.call-done) | copy-start | bytes 1572868
  272.4 10.4 %collective-permute-start.9 = (f32[32,1,128]{2,1,0:T(1,128)S(1)}, f32[32,1,128]{2,1,0:T(1,128)S(1)}, u32[]{:S(2)}, u32[]{:S(2)}) collective-permute-start(f32[32,1,128]{2,1,0:T(1,128)S(1)} %get-tuple-element.34), channel_id=1, source_target_pairs={{0,1},{1,2},{2,3},{4,5},{5,6},{6,7},{8,9},{9,10},{10,11},{12,13},{... | collective-permute-start | bytes 49160 | tf_op jit(solution)/shard_map/ppermute | solution.py:15
  274.1 8.6 %collective-permute-start.8 = (f32[32,1,128]{2,1,0:T(1,128)S(1)}, f32[32,1,128]{2,1,0:T(1,128)S(1)}, u32[]{:S(2)}, u32[]{:S(2)}) collective-permute-start(f32[32,1,128]{2,1,0:T(1,128)S(1)} %get-tuple-element.35), channel_id=1, source_target_pairs={{1,0},{2,1},{3,2},{5,4},{6,5},{7,6},{9,8},{10,9},{11,10},{13,12},{... | collective-permute-start | bytes 49160 | tf_op jit(solution)/shard_map/ppermute | solution.py:18
  282.7 89.6 %all-reduce.33.cloned.1.call-start = ((), (), s32[]{:S(2)}) async-start(), calls=%async_computation.6 | async-start | bytes 1048576 | tf_op jit(solution)/shard_map/psum | solution.py:51
  335.6 89.7 %all-reduce.35.cloned.1.call-start = ((), (), s32[]{:S(2)}) async-start(), calls=%async_computation.7 | async-start | bytes 294912 | tf_op jit(solution)/shard_map/psum | solution.py:39
  335.8 2.6 collective-permute-start.11
  337.1 4.6 collective-permute-start.10
  381.0 10.6 %collective-permute-start.13 = (f32[32,1,128]{2,1,0:T(1,128)S(1)}, f32[32,1,128]{2,1,0:T(1,128)S(1)}, u32[]{:S(2)}, u32[]{:S(2)}) collective-permute-start(f32[32,1,128]{2,1,0:T(1,128)S(1)} %get-tuple-element.30), channel_id=1, source_target_pairs={{0,1},{1,2},{2,3},{4,5},{5,6},{6,7},{8,9},{9,10},{10,11},{12,13},{... | collective-permute-start | bytes 49160 | tf_op jit(solution)/shard_map/ppermute | solution.py:15
  382.8 8.8 %collective-permute-start.12 = (f32[32,1,128]{2,1,0:T(1,128)S(1)}, f32[32,1,128]{2,1,0:T(1,128)S(1)}, u32[]{:S(2)}, u32[]{:S(2)}) collective-permute-start(f32[32,1,128]{2,1,0:T(1,128)S(1)} %get-tuple-element.31), channel_id=1, source_target_pairs={{1,0},{2,1},{3,2},{5,4},{6,5},{7,6},{9,8},{10,9},{11,10},{13,12},{... | collective-permute-start | bytes 49160 | tf_op jit(solution)/shard_map/ppermute | solution.py:18
  391.5 91.2 %all-reduce.37.cloned.1.call-start = ((), (), s32[]{:S(2)}) async-start(), calls=%async_computation.8 | async-start | bytes 1048576 | tf_op jit(solution)/shard_map/psum | solution.py:51
  392.2 45.9 %copy-start.2 = (f32[32,1152]{1,0:T(8,128)S(1)}, f32[32,1152]{1,0:T(8,128)}, u32[]{:S(2)}) copy-start(f32[32,1152]{1,0:T(8,128)} %all-reduce.31.cloned.1.call-done) | copy-start | bytes 442372
  439.1 0.7 copy-start.7
  439.8 6.4 %copy-start.3 = (f32[32,32,128]{2,1,0:T(8,128)S(1)}, f32[32,32,128]{2,1,0:T(8,128)}, u32[]{:S(2)}) copy-start(f32[32,32,128]{2,1,0:T(8,128)} %get-tuple-element.7) | copy-start | bytes 1572868
  446.1 88.5 %all-reduce.39.cloned.1.call-start = ((), (), s32[]{:S(2)}) async-start(), calls=%async_computation.9 | async-start | bytes 294912 | tf_op jit(solution)/shard_map/psum | solution.py:39
  446.3 2.6 collective-permute-start.15
  447.6 4.6 collective-permute-start.14
  482.7 7.2 %copy-start.1 = (f32[32,4096]{1,0:T(8,128)S(1)}, f32[32,4096]{1,0:T(8,128)}, u32[]{:S(2)}) copy-start(f32[32,4096]{1,0:T(8,128)} %all-reduce.37.cloned.1.call-done) | copy-start | bytes 1572868
  490.5 10.3 %collective-permute-start.17 = (f32[32,1,128]{2,1,0:T(1,128)S(1)}, f32[32,1,128]{2,1,0:T(1,128)S(1)}, u32[]{:S(2)}, u32[]{:S(2)}) collective-permute-start(f32[32,1,128]{2,1,0:T(1,128)S(1)} %get-tuple-element.26), channel_id=1, source_target_pairs={{0,1},{1,2},{2,3},{4,5},{5,6},{6,7},{8,9},{9,10},{10,11},{12,13},{... | collective-permute-start | bytes 49160 | tf_op jit(solution)/shard_map/ppermute | solution.py:15
  492.2 8.6 %collective-permute-start.16 = (f32[32,1,128]{2,1,0:T(1,128)S(1)}, f32[32,1,128]{2,1,0:T(1,128)S(1)}, u32[]{:S(2)}, u32[]{:S(2)}) collective-permute-start(f32[32,1,128]{2,1,0:T(1,128)S(1)} %get-tuple-element.27), channel_id=1, source_target_pairs={{1,0},{2,1},{3,2},{5,4},{6,5},{7,6},{9,8},{10,9},{11,10},{13,12},{... | collective-permute-start | bytes 49160 | tf_op jit(solution)/shard_map/ppermute | solution.py:18
  547.3 2.4 copy-start.8
  547.3 2.4 copy-start.10
Sparse Core Ops, SparseCore 0:
  13.6 41.2 all-reduce.20
  66.4 33.8 all-reduce.22
  119.6 36.4 all-reduce.24
  174.3 33.6 all-reduce.26
  228.1 36.4 all-reduce.28
  282.8 33.6 all-reduce.30
  335.8 36.4 all-reduce.32
  391.7 33.6 all-reduce.34
  446.2 36.4 all-reduce.36
  500.9 33.6 all-reduce.38
where the time goes:
time: 559 us; the launch traced here: 557 us
  waiting for transfers between devices  294 us (53%)
  blocking collectives  123 us (22%)
  matrix products  67.6 us (12%)
  other arithmetic  30.8 us (6%)
  starting transfers between devices  25.8 us (5%)
  between operations  14.8 us (3%)
    psum x5, waiting for transfers between devices, backward_sum(): lax.psum(jnp.dot(rounded, green_matrix, preferred_element_type=jnp.float3...  160 us
    psum x5, waiting for transfers between devices, forward(): return lax.psum(partial_value, 'par')  121 us
    psum x5, blocking collectives, curvatures(): image_sq = lax.psum(local_image, 'pix')  58.5 us
    dot_general x5, matrix products, forward(): lax.dot_general(rounded, green_matrix, (((1,), (1,)), ((), ())), preferre...  36.2 us
    psum x4, blocking collectives, curvatures(): smooth_sq = lax.psum(local_smooth, 'par')  33.2 us
    dot_general x5, matrix products, backward_sum(): jnp.dot(rounded, green_matrix, preferred_element_type=jnp.float32)  31.5 us
    psum x5, blocking collectives, column_squares(): return lax.psum(jnp.sum(gradient * gradient, axis=1), 'par')  31.1 us
    ppermute x9, starting transfers between devices, padded_2(): lax.ppermute(lax.slice_in_dim(block, block.shape[dim] - width, None, axis...  13.5 us
  transfers between devices with their start and end apart: 28, of which 14 were waited for; matrix products, arithmetic and copies ran while one was open for 8% of the time, Pallas kernels for 0%

commit v1 on v0

--- a/solution.py
+++ b/solution.py
@@ -1,10 +1,15 @@
+import functools
+
 import jax
 import jax.numpy as jnp
 from jax import lax
+from jax.experimental import pallas as pl
+from jax.experimental.pallas import tpu as pltpu
 from jax.sharding import PartitionSpec as P
 
 GRID = 128
 ITERS = 5
+LANES = 128
 
 
 def padded_2(block, sides, width):
@@ -82,9 +87,367 @@
     return (solution, residual)
 
 
+MESH = pl.DeviceIdType.MESH
+
+
+def to_row(column):
+    count = column.shape[0]
+    eye = lax.broadcasted_iota(jnp.int32, (count, LANES), 0) == lax.broadcasted_iota(
+        jnp.int32, (count, LANES), 1
+    )
+    return jnp.sum(jnp.where(eye, jnp.broadcast_to(column, (count, LANES)), 0.0), axis=0, keepdims=True)
+
+
+def to_column(row, count):
+    eye = lax.broadcasted_iota(jnp.int32, (count, LANES), 0) == lax.broadcasted_iota(
+        jnp.int32, (count, LANES), 1
+    )
+    return jnp.sum(jnp.where(eye, jnp.broadcast_to(row, (count, LANES)), 0.0), axis=1, keepdims=True)
+
+
+def stencil(above, here, below):
+    lane = lax.broadcasted_iota(jnp.int32, here.shape, 1)
+    left = jnp.where(lane == 0, 0.0, pltpu.roll(here, 1, 1))
+    right = jnp.where(lane == GRID - 1, 0.0, pltpu.roll(here, GRID - 1, 1))
+    return here - 0.25 * (above + below + left + right)
+
+
+def cgls_kernel(
+    nz, npar,
+    green_hbm, obs_ref, x_ref, r_ref,
+    green, imb, im, p_ext, sp, g_own, gg_ref,
+    rs_send, rs_recv, ag, y_send, y_recv, h_recv, halo,
+    sz, sp_scalar, nz_scalar, npar_scalar,
+    load_sem, rs_ss, rs_rs, ag_ss, ag_rs, y_ss, y_rs, h_ss, h_rs, halo_ss, halo_rs,
+    sz_ss, sz_rs, sp_ss, sp_rs, nz_ss, nz_rs, np_ss, np_rs,
+):
+    me_z = lax.axis_index("pix")
+    me_p = lax.axis_index("par")
+    core = lax.rem(me_p, 2)
+    chip = me_p // 2
+    nchip = npar // 2
+    partner = me_p + 1 - 2 * core
+    sets = obs_ref.shape[0]
+    half = sets // 2
+    width = green.shape[2]
+    rows = nz * width // GRID
+    own_rows = width // GRID
+    edge = 2 * GRID
+
+    loads = [
+        pltpu.make_async_copy(green_hbm.at[:, pl.ds(c * width, width)], green.at[c], load_sem.at[c])
+        for c in range(nz)
+    ]
+    for c in range(nz):
+        loads[c].start()
+
+    barrier = pltpu.get_barrier_semaphore()
+    for j in range(1, nz):
+        pl.semaphore_signal(barrier, inc=1, device_id={"pix": lax.rem(me_z + j, nz)}, device_id_type=MESH)
+    for j in range(1, npar):
+        pl.semaphore_signal(barrier, inc=1, device_id={"par": lax.rem(me_p + j, npar)}, device_id_type=MESH)
+
+    imb[...] = obs_ref[...]
+    im[...] = jnp.zeros_like(im)
+    p_ext[...] = jnp.zeros_like(p_ext)
+    g_own[...] = jnp.zeros_like(g_own)
+    gg_ref[...] = jnp.zeros_like(gg_ref)
+    x_ref[...] = jnp.zeros_like(x_ref)
+    r_ref[...] = obs_ref[...].astype(jnp.float32)
+
+    pl.semaphore_wait(barrier, nz + npar - 2)
+    for c in range(nz):
+        loads[c].wait()
+
+    def to_z(buf, k, ssem, rsem, peer):
+        return pltpu.make_async_remote_copy(
+            src_ref=buf.at[k, me_z], dst_ref=buf.at[k, me_z],
+            send_sem=ssem.at[k, peer], recv_sem=rsem.at[k, me_z],
+            device_id={"pix": peer}, device_id_type=MESH,
+        )
+
+    def from_z(buf, k, ssem, rsem, peer):
+        return pltpu.make_async_remote_copy(
+            src_ref=buf.at[k, peer], dst_ref=buf.at[k, peer],
+            send_sem=ssem.at[k, peer], recv_sem=rsem.at[k, peer],
+            device_id={"pix": peer}, device_id_type=MESH,
+        )
+
+    def to_par(buf, k, ssem, rsem, peer):
+        return pltpu.make_async_remote_copy(
+            src_ref=buf.at[k, me_p], dst_ref=buf.at[k, me_p],
+            send_sem=ssem.at[k, peer], recv_sem=rsem.at[k, me_p],
+            device_id={"par": peer}, device_id_type=MESH,
+        )
+
+    def from_par(buf, k, ssem, rsem, peer):
+        return pltpu.make_async_remote_copy(
+            src_ref=buf.at[k, peer], dst_ref=buf.at[k, peer],
+            send_sem=ssem.at[k, peer], recv_sem=rsem.at[k, peer],
+            device_id={"par": peer}, device_id_type=MESH,
+        )
+
+    z_peers = [lax.rem(me_z + j, nz) for j in range(1, nz)]
+    z_from = [lax.rem(me_z + nz - j, nz) for j in range(1, nz)]
+    p_peers = [lax.rem(me_p + j, npar) for j in range(1, npar)]
+
+    def total_row(buf, k, count):
+        value = buf[k, 0, 0:1]
+        for i in range(1, count):
+            value = value + buf[k, i, 0:1]
+        return value
+
+    def send_image_sq(k):
+        image = im[...]
+        row = to_row(jnp.sum(image * image, axis=1, keepdims=True))
+        sz[k, me_z] = jnp.broadcast_to(row, (8, LANES))
+        for peer in z_peers:
+            to_z(sz, k, sz_ss, sz_rs, peer).start()
+
+    def send_smooth_sq(k):
+        square = jnp.zeros((sets, GRID), jnp.float32)
+        for i in range(rows + 2):
+            line = stencil(
+                p_ext[:, i * GRID:(i + 1) * GRID],
+                p_ext[:, (i + 1) * GRID:(i + 2) * GRID],
+                p_ext[:, (i + 2) * GRID:(i + 3) * GRID],
+            )
+            if i == 0:
+                line = jnp.where(me_p == 0, 0.0, line)
+            elif i == rows + 1:
+                line = jnp.where(me_p == npar - 1, 0.0, line)
+            else:
+                square = square + line * line
+            sp[:, i * GRID:(i + 1) * GRID] = line
+        row = to_row(jnp.sum(square, axis=1, keepdims=True))
+        sp_scalar[k, me_p] = jnp.broadcast_to(row, (8, LANES))
+        for peer in p_peers:
+            to_par(sp_scalar, k, sp_ss, sp_rs, peer).start()
+
+    def curvature(k):
+        for peer in p_peers:
+            from_par(sp_scalar, k, sp_ss, sp_rs, peer).wait_recv()
+        for peer in z_from:
+            from_z(sz, k, sz_ss, sz_rs, peer).wait_recv()
+        return total_row(sz, k, nz) + total_row(sp_scalar, k, npar)
+
+    def apply_step(step):
+        x_ref[...] += step * p_ext[:, edge:edge + rows * GRID]
+        r_ref[...] -= step * im[...]
+
+    def finish_scalars(k):
+        for peer in z_peers:
+            to_z(sz, k, sz_ss, sz_rs, peer).wait_send()
+        for peer in p_peers:
+            to_par(sp_scalar, k, sp_ss, sp_rs, peer).wait_send()
+
+    def rs_copy(k, target):
+        return pltpu.make_async_remote_copy(
+            src_ref=rs_send.at[k, target], dst_ref=rs_recv.at[k, me_z],
+            send_sem=rs_ss.at[k, target], recv_sem=rs_rs.at[k, me_z],
+            device_id={"pix": target}, device_id_type=MESH,
+        )
+
+    def rs_from(k, source):
+        return pltpu.make_async_remote_copy(
+            src_ref=rs_send.at[k, source], dst_ref=rs_recv.at[k, source],
+            send_sem=rs_ss.at[k, source], recv_sem=rs_rs.at[k, source],
+            device_id={"pix": source}, device_id_type=MESH,
+        )
+
+    up = lax.rem(me_p + 1, npar)
+    down = lax.rem(me_p + npar - 1, npar)
+
+    def halo_copies(k):
+        return (
+            pltpu.make_async_remote_copy(
+                src_ref=ag.at[k, nz - 1, :, pl.ds(width - edge, edge)], dst_ref=halo.at[k, 0],
+                send_sem=halo_ss.at[k, 0], recv_sem=halo_rs.at[k, 0],
+                device_id={"par": up}, device_id_type=MESH,
+            ),
+            pltpu.make_async_remote_copy(
+                src_ref=ag.at[k, 0, :, pl.ds(0, edge)], dst_ref=halo.at[k, 1],
+                send_sem=halo_ss.at[k, 1], recv_sem=halo_rs.at[k, 1],
+                device_id={"par": down}, device_id_type=MESH,
+            ),
+        )
+
+    def y_copy(k):
+        return pltpu.make_async_remote_copy(
+            src_ref=y_send.at[k], dst_ref=y_recv.at[k],
+            send_sem=y_ss.at[k], recv_sem=y_rs.at[k],
+            device_id={"par": partner}, device_id_type=MESH,
+        )
+
+    @pl.loop(0, ITERS)
+    def _(k):
+        send_image_sq(k)
+        vector = imb[...]
+        for peer in z_peers:
+            rs_send[k, peer] = jnp.dot(
+                vector, green[peer], preferred_element_type=jnp.float32
+            ).astype(jnp.bfloat16)
+            rs_copy(k, peer).start()
+        send_smooth_sq(k)
+        fresh = jnp.dot(vector, green[me_z], preferred_element_type=jnp.float32)
+        base = me_z * own_rows
+        lines = []
+        for i in range(own_rows):
+            lines.append(stencil(*[
+                sp[:, pl.ds(pl.multiple_of((base + i + d) * GRID, GRID), GRID)] for d in range(3)
+            ]))
+        fresh = fresh + jnp.concatenate(lines, axis=1)
+        step = jnp.where(k == 0, -1.0, gg_ref[0:1] / curvature(k))
+        step = to_column(step, sets)
+        apply_step(step)
+        for source in z_from:
+            rs_from(k, source).wait_recv()
+            fresh = fresh + rs_recv[k, source].astype(jnp.float32)
+        gradient = g_own[...] - step * fresh
+        g_own[...] = gradient
+        ag[k, me_z] = gradient.astype(jnp.bfloat16)
+        for peer in z_peers:
+            to_z(ag, k, ag_ss, ag_rs, peer).start()
+        row = to_row(jnp.sum(gradient * gradient, axis=1, keepdims=True))
+        nz_scalar[k, me_z] = jnp.broadcast_to(row, (8, LANES))
+        for peer in z_peers:
+            to_z(nz_scalar, k, nz_ss, nz_rs, peer).start()
+
+        def forward(index):
+            return lax.dot_general(
+                ag[k, index], green[index], (((1,), (1,)), ((), ())),
+                preferred_element_type=jnp.float32,
+            )
+
+        image = forward(me_z)
+        for source in z_from:
+            from_z(ag, k, ag_ss, ag_rs, source).wait_recv()
+            image = image + forward(source)
+        for source in z_from:
+            from_z(nz_scalar, k, nz_ss, nz_rs, source).wait_recv()
+        low, high = image[:half], image[half:]
+        mine = jnp.where(core == 0, low, high)
+        y_send[k] = jnp.where(core == 0, high, low).astype(jnp.bfloat16)
+        y_copy(k).start()
+        npar_scalar[k, me_p] = jnp.broadcast_to(total_row(nz_scalar, k, nz), (8, LANES))
+        for peer in p_peers:
+            to_par(npar_scalar, k, np_ss, np_rs, peer).start()
+        for copy in halo_copies(k):
+            copy.start()
+        y_copy(k).wait_recv()
+        h_recv[k, me_p] = (mine + y_recv[k].astype(jnp.float32)).astype(jnp.bfloat16)
+        for peer in p_peers:
+            to_par(h_recv, k, h_ss, h_rs, peer).start()
+
+        for peer in p_peers:
+            from_par(npar_scalar, k, np_ss, np_rs, peer).wait_recv()
+        fresh_sq = total_row(npar_scalar, k, npar)
+        ratio = to_column(jnp.where(k == 0, 0.0, fresh_sq / gg_ref[0:1]), sets)
+        gg_ref[...] = jnp.broadcast_to(fresh_sq, gg_ref.shape)
+        for copy in halo_copies(k):
+            copy.wait_recv()
+        for c in range(nz):
+            where = slice(edge + c * width, edge + (c + 1) * width)
+            p_ext[:, where] = ag[k, c].astype(jnp.float32) + ratio * p_ext[:, where]
+        first = jnp.where(me_p == 0, 0.0, halo[k, 0].astype(jnp.float32))
+        p_ext[:, :edge] = first + ratio * p_ext[:, :edge]
+        last = jnp.where(me_p == npar - 1, 0.0, halo[k, 1].astype(jnp.float32))
+        p_ext[:, edge + rows * GRID:] = last + ratio * p_ext[:, edge + rows * GRID:]
+
+        for peer in p_peers:
+            from_par(h_recv, k, h_ss, h_rs, peer).wait_recv()
+        for c in range(2):
+            part = h_recv[k, c].astype(jnp.float32)
+            for i in range(1, nchip):
+                part = part + h_recv[k, 2 * i + c].astype(jnp.float32)
+            where = slice(c * half, (c + 1) * half)
+            im[where] = part + ratio[where] * im[where]
+        imb[...] = im[...].astype(jnp.bfloat16)
+
+        finish_scalars(k)
+        for peer in z_peers:
+            rs_copy(k, peer).wait_send()
+            to_z(ag, k, ag_ss, ag_rs, peer).wait_send()
+            to_z(nz_scalar, k, nz_ss, nz_rs, peer).wait_send()
+        y_copy(k).wait_send()
+        for copy in halo_copies(k):
+            copy.wait_send()
+        for peer in p_peers:
+            to_par(npar_scalar, k, np_ss, np_rs, peer).wait_send()
+            to_par(h_recv, k, h_ss, h_rs, peer).wait_send()
+
+    send_image_sq(ITERS)
+    send_smooth_sq(ITERS)
+    step = to_column(gg_ref[0:1] / curvature(ITERS), sets)
+    apply_step(step)
+    finish_scalars(ITERS)
+
+
+def on_device_kernel(nz, npar, green_matrix, observed):
+    sets, pixels = observed.shape
+    cells = green_matrix.shape[1]
+    width = cells // nz
+    half = sets // 2
+    bf16, f32 = jnp.bfloat16, jnp.float32
+    dma = pltpu.SemaphoreType.DMA
+    n = ITERS
+    vmem = pl.BlockSpec(memory_space=pltpu.VMEM)
+    return pl.pallas_call(
+        functools.partial(cgls_kernel, nz, npar),
+        out_shape=(
+            jax.ShapeDtypeStruct((sets, cells), f32),
+            jax.ShapeDtypeStruct((sets, pixels), f32),
+        ),
+        in_specs=[pl.BlockSpec(memory_space=pl.ANY), vmem],
+        out_specs=(vmem, vmem),
+        scratch_shapes=[
+            pltpu.VMEM((nz, pixels, width), bf16),
+            pltpu.VMEM((sets, pixels), bf16),
+            pltpu.VMEM((sets, pixels), f32),
+            pltpu.VMEM((sets, cells + 4 * GRID), f32),
+            pltpu.VMEM((sets, cells + 2 * GRID), f32),
+            pltpu.VMEM((sets, width), f32),
+            pltpu.VMEM((8, LANES), f32),
+            pltpu.VMEM((n, nz, sets, width), bf16),
+            pltpu.VMEM((n, nz, sets, width), bf16),
+            pltpu.VMEM((n, nz, sets, width), bf16),
+            pltpu.VMEM((n, half, pixels), bf16),
+            pltpu.VMEM((n, half, pixels), bf16),
+            pltpu.VMEM((n, npar, half, pixels), bf16),
+            pltpu.VMEM((n, 2, sets, 2 * GRID), bf16),
+            pltpu.VMEM((n + 1, nz, 8, LANES), f32),
+            pltpu.VMEM((n + 1, npar, 8, LANES), f32),
+            pltpu.VMEM((n, nz, 8, LANES), f32),
+            pltpu.VMEM((n, npar, 8, LANES), f32),
+            dma((nz,)),
+            dma((n, nz)), dma((n, nz)),
+            dma((n, nz)), dma((n, nz)),
+            dma((n,)), dma((n,)),
+            dma((n, npar)), dma((n, npar)),
+            dma((n, 2)), dma((n, 2)),
+            dma((n + 1, nz)), dma((n + 1, nz)),
+            dma((n + 1, npar)), dma((n + 1, npar)),
+            dma((n, nz)), dma((n, nz)),
+            dma((n, npar)), dma((n, npar)),
+        ],
+        compiler_params=pltpu.CompilerParams(
+            collective_id=0, has_side_effects=True, vmem_limit_bytes=60 * 1024 * 1024
+        ),
+    )(green_matrix, observed)
+
+
 def solution(mesh):
+    nz, npar = mesh.shape["pix"], mesh.shape["par"]
+
+    def step(green_matrix, observed):
+        sets, cells = observed.shape[0], green_matrix.shape[1]
+        fits = cells % (nz * GRID) == 0 and cells // nz >= 2 * GRID
+        if fits and nz > 1 and npar % 2 == 0 and sets % 32 == 0 and sets <= LANES:
+            return on_device_kernel(nz, npar, green_matrix, observed)
+        return on_device(green_matrix, observed)
+
     return jax.shard_map(
-        on_device,
+        step,
         mesh=mesh,
         in_specs=(P("pix", "par"), P("parts", "pix")),
         out_specs=(P("parts", "par"), P("parts", "pix")),

time: 559 us -> 137 us (0.25)
  waiting for transfers between devices: 294 us -> 0 us
  Pallas kernels: 0 us -> 132 us
  blocking collectives: 123 us -> 0 us
  matrix products: 67.6 us -> 0 us
  other arithmetic: 30.8 us -> 0 us
  starting transfers between devices: 25.8 us -> 0 us
  between operations: 14.8 us -> 0.64 us
    psum x10 -> x0, waiting for transfers between devices: 281 us -> none  [the longest x5 160 us: backward_sum(): lax.psum(jnp.dot(rounded, green_matrix, preferred_element_type=jnp.float3...]
    pallas_call x0 -> x1, Pallas kernels: none -> 132 us  [on_device_kernel(): pl.pallas_call(functools.partial(cgls_kernel, nz, npar), out_shape=(jax.S...]
    psum x14 -> x0, blocking collectives: 123 us -> none  [the longest x5 58.5 us: curvatures(): image_sq = lax.psum(local_image, 'pix')]
    dot_general x10 -> x0, matrix products: 67.6 us -> none  [the longest x5 36.2 us: forward(): lax.dot_general(rounded, green_matrix, (((1,), (1,)), ((), ())), preferre...]
    ppermute x18 -> x0, starting transfers between devices: 25.4 us -> none  [the longest x9 13.5 us: padded_2(): lax.ppermute(lax.slice_in_dim(block, block.shape[dim] - width, None, axis...]
    reduce_sum x15 -> x0, other arithmetic: 16 us -> none  [the longest x5 7.39 us: column_squares(): return lax.psum(jnp.sum(gradient * gradient, axis=1), 'par')]
    ppermute x18 -> x0, waiting for transfers between devices: 13.2 us -> none  [the longest x9 13.1 us: padded_2(): lax.ppermute(lax.slice_in_dim(block, 0, width, axis=dim), axis, backward)]
  transfers between devices with their start and end apart: 28 -> 0, of which waited for: 14 -> 0; matrix products, arithmetic and copies ran while one was open for 8% -> 0% of each run, Pallas kernels for 0% -> 0%
where the time goes in v1:
time: 137 us
  Pallas kernels  132 us (96%)
  local copies, waits for them, and re-layouts  3.45 us (3%)
    pallas_call x1, Pallas kernels, on_device_kernel(): pl.pallas_call(functools.partial(cgls_kernel, nz, npar), out_shape=(jax.S...  132 us
    unnamed x2, local copies, waits for them, and re-layouts  3.45 us

profile of v1, /device:TPU:0, one launch (start us, length us, event | category | flops | bytes accessed | tf_op | source)
XLA Modules:
  0.0 136.6 jit_solution(10263425555475613687)
XLA Ops:
  0.6 132.5 %shard_map.41 = (f32[32,4096]{1,0:T(8,128)}, f32[32,1152]{1,0:T(8,128)}) custom-call(bf16[1152,4096]{1,0:T(8,128)(2,1)} %green_hbm.1, bf16[32,1152]{1,0:T(8,128)(2,1)} %obs_ref.1), custom_call_target="tpu_custom_call" | custom-call | tf_op jit(solution)/shard_map/pallas_call | solution.py:395
  133.1 1.9 %copy.6 = f32[32,4096]{1,0:T(8,128)} copy(f32[32,4096]{1,0:T(8,128)} %get-tuple-element.4) | data formatting | bytes 1048576
  135.0 1.6 %copy.7 = f32[32,1152]{1,0:T(8,128)} copy(f32[32,1152]{1,0:T(8,128)} %get-tuple-element.5) | data formatting | bytes 294912

commit v2 on v1

--- a/solution.py
+++ b/solution.py
@@ -10,6 +10,7 @@
 GRID = 128
 ITERS = 5
 LANES = 128
+SUB = 2
 
 
 def padded_2(block, sides, width):
@@ -105,6 +106,24 @@
     return jnp.sum(jnp.where(eye, jnp.broadcast_to(row, (count, LANES)), 0.0), axis=1, keepdims=True)
 
 
+def flipped(index, mask, count):
+    value, bit = 0, 1
+    while bit < count:
+        digit = lax.rem(index // bit, 2)
+        value = value + bit * (1 - digit if mask & bit else digit)
+        bit *= 2
+    return value
+
+
+def far_first(count):
+    masks = []
+    bit = count // 2
+    while bit:
+        masks += range(bit, 2 * bit)
+        bit //= 2
+    return masks
+
+
 def stencil(above, here, below):
     lane = lax.broadcasted_iota(jnp.int32, here.shape, 1)
     left = jnp.where(lane == 0, 0.0, pltpu.roll(here, 1, 1))
@@ -115,7 +134,7 @@
 def cgls_kernel(
     nz, npar,
     green_hbm, obs_ref, x_ref, r_ref,
-    green, imb, im, p_ext, sp, g_own, gg_ref,
+    green, imb, im, p_ext, sp, g_own, own_part, gg_ref,
     rs_send, rs_recv, ag, y_send, y_recv, h_recv, halo,
     sz, sp_scalar, nz_scalar, npar_scalar,
     load_sem, rs_ss, rs_rs, ag_ss, ag_rs, y_ss, y_rs, h_ss, h_rs, halo_ss, halo_rs,
@@ -129,17 +148,23 @@
     partner = me_p + 1 - 2 * core
     sets = obs_ref.shape[0]
     half = sets // 2
-    width = green.shape[2]
-    rows = nz * width // GRID
+    width = green.shape[3]
+    rows = nz * SUB * width // GRID
     own_rows = width // GRID
     edge = 2 * GRID
-
-    loads = [
-        pltpu.make_async_copy(green_hbm.at[:, pl.ds(c * width, width)], green.at[c], load_sem.at[c])
-        for c in range(nz)
-    ]
-    for c in range(nz):
-        loads[c].start()
+    z_peers = [flipped(me_z, mask, nz) for mask in far_first(nz)]
+    z_from = z_peers[::-1]
+    p_peers = [lax.rem(me_p + j, npar) for j in range(1, npar)]
+    order = [(s, c) for s in range(SUB) for c in z_peers] + [(s, me_z) for s in range(SUB)]
+
+    def load(s, c):
+        first = pl.multiple_of((c * SUB + s) * width, width)
+        return pltpu.make_async_copy(
+            green_hbm.at[:, pl.ds(first, width)], green.at[c, s], load_sem.at[c, s]
+        )
+
+    for s, c in order:
+        load(s, c).start()
 
     barrier = pltpu.get_barrier_semaphore()
     for j in range(1, nz):
@@ -156,20 +181,18 @@
     r_ref[...] = obs_ref[...].astype(jnp.float32)
 
     pl.semaphore_wait(barrier, nz + npar - 2)
-    for c in range(nz):
-        loads[c].wait()
-
-    def to_z(buf, k, ssem, rsem, peer):
-        return pltpu.make_async_remote_copy(
-            src_ref=buf.at[k, me_z], dst_ref=buf.at[k, me_z],
-            send_sem=ssem.at[k, peer], recv_sem=rsem.at[k, me_z],
+
+    def to_z(buf, k, ssem, rsem, peer, s=0):
+        return pltpu.make_async_remote_copy(
+            src_ref=buf.at[k, me_z, s], dst_ref=buf.at[k, me_z, s],
+            send_sem=ssem.at[k, peer, s], recv_sem=rsem.at[k, me_z, s],
             device_id={"pix": peer}, device_id_type=MESH,
         )
 
-    def from_z(buf, k, ssem, rsem, peer):
-        return pltpu.make_async_remote_copy(
-            src_ref=buf.at[k, peer], dst_ref=buf.at[k, peer],
-            send_sem=ssem.at[k, peer], recv_sem=rsem.at[k, peer],
+    def from_z(buf, k, ssem, rsem, peer, s=0):
+        return pltpu.make_async_remote_copy(
+            src_ref=buf.at[k, peer, s], dst_ref=buf.at[k, peer, s],
+            send_sem=ssem.at[k, peer, s], recv_sem=rsem.at[k, peer, s],
             device_id={"pix": peer}, device_id_type=MESH,
         )
 
@@ -187,20 +210,23 @@
             device_id={"par": peer}, device_id_type=MESH,
         )
 
-    z_peers = [lax.rem(me_z + j, nz) for j in range(1, nz)]
-    z_from = [lax.rem(me_z + nz - j, nz) for j in range(1, nz)]
-    p_peers = [lax.rem(me_p + j, npar) for j in range(1, npar)]
-
-    def total_row(buf, k, count):
-        value = buf[k, 0, 0:1]
-        for i in range(1, count):
-            value = value + buf[k, i, 0:1]
+
+    def total_row(parts):
+        value = parts[0]
+        for part in parts[1:]:
+            value = value + part
         return value
+
+    def z_row(buf, k):
+        return total_row([buf[k, i, 0, 0:1] for i in range(nz)])
+
+    def par_row(buf, k):
+        return total_row([buf[k, i, 0:1] for i in range(npar)])
 
     def send_image_sq(k):
         image = im[...]
         row = to_row(jnp.sum(image * image, axis=1, keepdims=True))
-        sz[k, me_z] = jnp.broadcast_to(row, (8, LANES))
+        sz[k, me_z, 0] = jnp.broadcast_to(row, (8, LANES))
         for peer in z_peers:
             to_z(sz, k, sz_ss, sz_rs, peer).start()
 
@@ -229,7 +255,7 @@
             from_par(sp_scalar, k, sp_ss, sp_rs, peer).wait_recv()
         for peer in z_from:
             from_z(sz, k, sz_ss, sz_rs, peer).wait_recv()
-        return total_row(sz, k, nz) + total_row(sp_scalar, k, npar)
+        return z_row(sz, k) + par_row(sp_scalar, k)
 
     def apply_step(step):
         x_ref[...] += step * p_ext[:, edge:edge + rows * GRID]
@@ -241,17 +267,17 @@
         for peer in p_peers:
             to_par(sp_scalar, k, sp_ss, sp_rs, peer).wait_send()
 
-    def rs_copy(k, target):
-        return pltpu.make_async_remote_copy(
-            src_ref=rs_send.at[k, target], dst_ref=rs_recv.at[k, me_z],
-            send_sem=rs_ss.at[k, target], recv_sem=rs_rs.at[k, me_z],
+    def rs_copy(k, target, s):
+        return pltpu.make_async_remote_copy(
+            src_ref=rs_send.at[k, target, s], dst_ref=rs_recv.at[k, me_z, s],
+            send_sem=rs_ss.at[k, target, s], recv_sem=rs_rs.at[k, me_z, s],
             device_id={"pix": target}, device_id_type=MESH,
         )
 
-    def rs_from(k, source):
-        return pltpu.make_async_remote_copy(
-            src_ref=rs_send.at[k, source], dst_ref=rs_recv.at[k, source],
-            send_sem=rs_ss.at[k, source], recv_sem=rs_rs.at[k, source],
+    def rs_from(k, source, s):
+        return pltpu.make_async_remote_copy(
+            src_ref=rs_send.at[k, source, s], dst_ref=rs_recv.at[k, source, s],
+            send_sem=rs_ss.at[k, source, s], recv_sem=rs_rs.at[k, source, s],
             device_id={"pix": source}, device_id_type=MESH,
         )
 
@@ -261,12 +287,12 @@
     def halo_copies(k):
         return (
             pltpu.make_async_remote_copy(
-                src_ref=ag.at[k, nz - 1, :, pl.ds(width - edge, edge)], dst_ref=halo.at[k, 0],
+                src_ref=ag.at[k, nz - 1, SUB - 1, :, pl.ds(width - edge, edge)], dst_ref=halo.at[k, 0],
                 send_sem=halo_ss.at[k, 0], recv_sem=halo_rs.at[k, 0],
                 device_id={"par": up}, device_id_type=MESH,
             ),
             pltpu.make_async_remote_copy(
-                src_ref=ag.at[k, 0, :, pl.ds(0, edge)], dst_ref=halo.at[k, 1],
+                src_ref=ag.at[k, 0, 0, :, pl.ds(0, edge)], dst_ref=halo.at[k, 1],
                 send_sem=halo_ss.at[k, 1], recv_sem=halo_rs.at[k, 1],
                 device_id={"par": down}, device_id_type=MESH,
             ),
@@ -283,53 +309,67 @@
     def _(k):
         send_image_sq(k)
         vector = imb[...]
-        for peer in z_peers:
-            rs_send[k, peer] = jnp.dot(
-                vector, green[peer], preferred_element_type=jnp.float32
-            ).astype(jnp.bfloat16)
-            rs_copy(k, peer).start()
+
+        def backward(s, c):
+            @pl.when(k == 0)
+            def _():
+                load(s, c).wait()
+
+            return jnp.dot(vector, green[c, s], preferred_element_type=jnp.float32)
+
+        for s in range(SUB):
+            for peer in z_peers:
+                rs_send[k, peer, s] = backward(s, peer).astype(jnp.bfloat16)
+                rs_copy(k, peer, s).start()
         send_smooth_sq(k)
-        fresh = jnp.dot(vector, green[me_z], preferred_element_type=jnp.float32)
-        base = me_z * own_rows
-        lines = []
-        for i in range(own_rows):
-            lines.append(stencil(*[
-                sp[:, pl.ds(pl.multiple_of((base + i + d) * GRID, GRID), GRID)] for d in range(3)
-            ]))
-        fresh = fresh + jnp.concatenate(lines, axis=1)
+        for s in range(SUB):
+            base = (me_z * SUB + s) * own_rows
+            lines = []
+            for i in range(own_rows):
+                lines.append(stencil(*[
+                    sp[:, pl.ds(pl.multiple_of((base + i + d) * GRID, GRID), GRID)]
+                    for d in range(3)
+                ]))
+            own_part[s] = backward(s, me_z) + jnp.concatenate(lines, axis=1)
         step = jnp.where(k == 0, -1.0, gg_ref[0:1] / curvature(k))
         step = to_column(step, sets)
-        apply_step(step)
-        for source in z_from:
-            rs_from(k, source).wait_recv()
-            fresh = fresh + rs_recv[k, source].astype(jnp.float32)
-        gradient = g_own[...] - step * fresh
-        g_own[...] = gradient
-        ag[k, me_z] = gradient.astype(jnp.bfloat16)
-        for peer in z_peers:
-            to_z(ag, k, ag_ss, ag_rs, peer).start()
-        row = to_row(jnp.sum(gradient * gradient, axis=1, keepdims=True))
-        nz_scalar[k, me_z] = jnp.broadcast_to(row, (8, LANES))
+        square = jnp.zeros((sets, 1), jnp.float32)
+        for s in range(SUB):
+            fresh = own_part[s]
+            for source in z_from:
+                rs_from(k, source, s).wait_recv()
+                fresh = fresh + rs_recv[k, source, s].astype(jnp.float32)
+            gradient = g_own[s] - step * fresh
+            g_own[s] = gradient
+            ag[k, me_z, s] = gradient.astype(jnp.bfloat16)
+            for peer in z_peers:
+                to_z(ag, k, ag_ss, ag_rs, peer, s).start()
+            square = square + jnp.sum(gradient * gradient, axis=1, keepdims=True)
+        nz_scalar[k, me_z, 0] = jnp.broadcast_to(to_row(square), (8, LANES))
         for peer in z_peers:
             to_z(nz_scalar, k, nz_ss, nz_rs, peer).start()
-
-        def forward(index):
+        apply_step(step)
+
+        def forward(s, c):
             return lax.dot_general(
-                ag[k, index], green[index], (((1,), (1,)), ((), ())),
+                ag[k, c, s], green[c, s], (((1,), (1,)), ((), ())),
                 preferred_element_type=jnp.float32,
             )
 
-        image = forward(me_z)
-        for source in z_from:
-            from_z(ag, k, ag_ss, ag_rs, source).wait_recv()
-            image = image + forward(source)
+        image = jnp.zeros(im.shape, jnp.float32)
+        for s in range(SUB):
+            image = image + forward(s, me_z)
+        for s in range(SUB):
+            for source in z_from:
+                from_z(ag, k, ag_ss, ag_rs, source, s).wait_recv()
+                image = image + forward(s, source)
         for source in z_from:
             from_z(nz_scalar, k, nz_ss, nz_rs, source).wait_recv()
         low, high = image[:half], image[half:]
         mine = jnp.where(core == 0, low, high)
         y_send[k] = jnp.where(core == 0, high, low).astype(jnp.bfloat16)
         y_copy(k).start()
-        npar_scalar[k, me_p] = jnp.broadcast_to(total_row(nz_scalar, k, nz), (8, LANES))
+        npar_scalar[k, me_p] = jnp.broadcast_to(z_row(nz_scalar, k), (8, LANES))
         for peer in p_peers:
             to_par(npar_scalar, k, np_ss, np_rs, peer).start()
         for copy in halo_copies(k):
@@ -341,14 +381,16 @@
 
         for peer in p_peers:
             from_par(npar_scalar, k, np_ss, np_rs, peer).wait_recv()
-        fresh_sq = total_row(npar_scalar, k, npar)
+        fresh_sq = par_row(npar_scalar, k)
         ratio = to_column(jnp.where(k == 0, 0.0, fresh_sq / gg_ref[0:1]), sets)
         gg_ref[...] = jnp.broadcast_to(fresh_sq, gg_ref.shape)
         for copy in halo_copies(k):
             copy.wait_recv()
         for c in range(nz):
-            where = slice(edge + c * width, edge + (c + 1) * width)
-            p_ext[:, where] = ag[k, c].astype(jnp.float32) + ratio * p_ext[:, where]
+            for s in range(SUB):
+                first = edge + (c * SUB + s) * width
+                where = slice(first, first + width)
+                p_ext[:, where] = ag[k, c, s].astype(jnp.float32) + ratio * p_ext[:, where]
         first = jnp.where(me_p == 0, 0.0, halo[k, 0].astype(jnp.float32))
         p_ext[:, :edge] = first + ratio * p_ext[:, :edge]
         last = jnp.where(me_p == npar - 1, 0.0, halo[k, 1].astype(jnp.float32))
@@ -366,8 +408,9 @@
 
         finish_scalars(k)
         for peer in z_peers:
-            rs_copy(k, peer).wait_send()
-            to_z(ag, k, ag_ss, ag_rs, peer).wait_send()
+            for s in range(SUB):
+                rs_copy(k, peer, s).wait_send()
+                to_z(ag, k, ag_ss, ag_rs, peer, s).wait_send()
             to_z(nz_scalar, k, nz_ss, nz_rs, peer).wait_send()
         y_copy(k).wait_send()
         for copy in halo_copies(k):
@@ -386,7 +429,7 @@
 def on_device_kernel(nz, npar, green_matrix, observed):
     sets, pixels = observed.shape
     cells = green_matrix.shape[1]
-    width = cells // nz
+    width = cells // (nz * SUB)
     half = sets // 2
     bf16, f32 = jnp.bfloat16, jnp.float32
     dma = pltpu.SemaphoreType.DMA
@@ -401,33 +444,34 @@
         in_specs=[pl.BlockSpec(memory_space=pl.ANY), vmem],
         out_specs=(vmem, vmem),
         scratch_shapes=[
-            pltpu.VMEM((nz, pixels, width), bf16),
+            pltpu.VMEM((nz, SUB, pixels, width), bf16),
             pltpu.VMEM((sets, pixels), bf16),
             pltpu.VMEM((sets, pixels), f32),
             pltpu.VMEM((sets, cells + 4 * GRID), f32),
             pltpu.VMEM((sets, cells + 2 * GRID), f32),
-            pltpu.VMEM((sets, width), f32),
+            pltpu.VMEM((SUB, sets, width), f32),
+            pltpu.VMEM((SUB, sets, width), f32),
             pltpu.VMEM((8, LANES), f32),
-            pltpu.VMEM((n, nz, sets, width), bf16),
-            pltpu.VMEM((n, nz, sets, width), bf16),
-            pltpu.VMEM((n, nz, sets, width), bf16),
+            pltpu.VMEM((n, nz, SUB, sets, width), bf16),
+            pltpu.VMEM((n, nz, SUB, sets, width), bf16),
+            pltpu.VMEM((n, nz, SUB, sets, width), bf16),
             pltpu.VMEM((n, half, pixels), bf16),
             pltpu.VMEM((n, half, pixels), bf16),
             pltpu.VMEM((n, npar, half, pixels), bf16),
             pltpu.VMEM((n, 2, sets, 2 * GRID), bf16),
-            pltpu.VMEM((n + 1, nz, 8, LANES), f32),
+            pltpu.VMEM((n + 1, nz, 1, 8, LANES), f32),
             pltpu.VMEM((n + 1, npar, 8, LANES), f32),
-            pltpu.VMEM((n, nz, 8, LANES), f32),
+            pltpu.VMEM((n, nz, 1, 8, LANES), f32),
             pltpu.VMEM((n, npar, 8, LANES), f32),
-            dma((nz,)),
-            dma((n, nz)), dma((n, nz)),
-            dma((n, nz)), dma((n, nz)),
+            dma((nz, SUB)),
+            dma((n, nz, SUB)), dma((n, nz, SUB)),
+            dma((n, nz, SUB)), dma((n, nz, SUB)),
             dma((n,)), dma((n,)),
             dma((n, npar)), dma((n, npar)),
             dma((n, 2)), dma((n, 2)),
-            dma((n + 1, nz)), dma((n + 1, nz)),
+            dma((n + 1, nz, 1)), dma((n + 1, nz, 1)),
             dma((n + 1, npar)), dma((n + 1, npar)),
-            dma((n, nz)), dma((n, nz)),
+            dma((n, nz, 1)), dma((n, nz, 1)),
             dma((n, npar)), dma((n, npar)),
         ],
         compiler_params=pltpu.CompilerParams(
@@ -441,7 +485,8 @@
 
     def step(green_matrix, observed):
         sets, cells = observed.shape[0], green_matrix.shape[1]
-        fits = cells % (nz * GRID) == 0 and cells // nz >= 2 * GRID
+        width = cells // (nz * SUB)
+        fits = cells % (nz * SUB * GRID) == 0 and width >= 2 * GRID and nz & (nz - 1) == 0
         if fits and nz > 1 and npar % 2 == 0 and sets % 32 == 0 and sets <= LANES:
             return on_device_kernel(nz, npar, green_matrix, observed)
         return on_device(green_matrix, observed)

time: 137 us -> 114 us (0.83)
  Pallas kernels: 132 us -> 110 us
    pallas_call x1, Pallas kernels: 132 us -> 110 us  [on_device_kernel(): pl.pallas_call(functools.partial(cgls_kernel, nz, npar), out_shape=(jax.S...]
where the time goes in v2:
time: 114 us
  Pallas kernels  110 us (96%)
  local copies, waits for them, and re-layouts  3.45 us (3%)
    pallas_call x1, Pallas kernels, on_device_kernel(): pl.pallas_call(functools.partial(cgls_kernel, nz, npar), out_shape=(jax.S...  110 us
    unnamed x2, local copies, waits for them, and re-layouts  3.45 us

profile of v2, /device:TPU:0, one launch (start us, length us, event | category | flops | bytes accessed | tf_op | source)
XLA Modules:
  0.0 113.7 jit_solution(11126538309107565598)
XLA Ops:
  0.6 109.6 %shard_map.41 = (f32[32,4096]{1,0:T(8,128)}, f32[32,1152]{1,0:T(8,128)}) custom-call(bf16[1152,4096]{1,0:T(8,128)(2,1)} %green_hbm.1, bf16[32,1152]{1,0:T(8,128)(2,1)} %obs_ref.1), custom_call_target="tpu_custom_call" | custom-call | tf_op jit(solution)/shard_map/pallas_call | solution.py:438
  110.3 1.9 %copy.6 = f32[32,4096]{1,0:T(8,128)} copy(f32[32,4096]{1,0:T(8,128)} %get-tuple-element.4) | data formatting | bytes 1048576
  112.1 1.6 %copy.7 = f32[32,1152]{1,0:T(8,128)} copy(f32[32,1152]{1,0:T(8,128)} %get-tuple-element.5) | data formatting | bytes 294912

commit v3 on v2

--- a/solution.py
+++ b/solution.py
@@ -137,7 +137,7 @@
     green, imb, im, p_ext, sp, g_own, own_part, gg_ref,
     rs_send, rs_recv, ag, y_send, y_recv, h_recv, halo,
     sz, sp_scalar, nz_scalar, npar_scalar,
-    load_sem, rs_ss, rs_rs, ag_ss, ag_rs, y_ss, y_rs, h_ss, h_rs, halo_ss, halo_rs,
+    load_sem, rs_ss, rs_rs, ag_ss, ag_rs, relay_ss, y_ss, y_rs, h_ss, h_rs, halo_ss, halo_rs,
     sz_ss, sz_rs, sp_ss, sp_rs, nz_ss, nz_rs, np_ss, np_rs,
 ):
     me_z = lax.axis_index("pix")
@@ -281,6 +281,24 @@
             device_id={"pix": source}, device_id_type=MESH,
         )
 
+    def relay_masks(s):
+        if s + 1 == SUB:
+            return []
+        return [mask for mask in far_first(nz) if mask % 2 == 0]
+
+    def sent_masks(s):
+        if s + 1 == SUB:
+            return far_first(nz)
+        return [mask for mask in far_first(nz) if mask % 2 == 0 or mask == 1]
+
+    def relay(k, source, s):
+        mate = flipped(me_z, 1, nz)
+        return pltpu.make_async_remote_copy(
+            src_ref=ag.at[k, source, s], dst_ref=ag.at[k, source, s],
+            send_sem=relay_ss.at[k, source, s], recv_sem=ag_rs.at[k, source, s],
+            device_id={"pix": mate}, device_id_type=MESH,
+        )
+
     up = lax.rem(me_p + 1, npar)
     down = lax.rem(me_p + npar - 1, npar)
 
@@ -342,8 +360,8 @@
             gradient = g_own[s] - step * fresh
             g_own[s] = gradient
             ag[k, me_z, s] = gradient.astype(jnp.bfloat16)
-            for peer in z_peers:
-                to_z(ag, k, ag_ss, ag_rs, peer, s).start()
+            for mask in sent_masks(s):
+                to_z(ag, k, ag_ss, ag_rs, flipped(me_z, mask, nz), s).start()
             square = square + jnp.sum(gradient * gradient, axis=1, keepdims=True)
         nz_scalar[k, me_z, 0] = jnp.broadcast_to(to_row(square), (8, LANES))
         for peer in z_peers:
@@ -360,15 +378,29 @@
         for s in range(SUB):
             image = image + forward(s, me_z)
         for s in range(SUB):
-            for source in z_from:
+            for mask in relay_masks(s):
+                source = flipped(me_z, mask, nz)
                 from_z(ag, k, ag_ss, ag_rs, source, s).wait_recv()
+                relay(k, source, s).start()
+        for s in range(SUB):
+            for mask in sent_masks(s)[::-1]:
+                source = flipped(me_z, mask, nz)
+                if mask not in relay_masks(s):
+                    from_z(ag, k, ag_ss, ag_rs, source, s).wait_recv()
                 image = image + forward(s, source)
-        for source in z_from:
-            from_z(nz_scalar, k, nz_ss, nz_rs, source).wait_recv()
+            if s + 2 <= SUB:
+                continue
+            for t in range(SUB):
+                for mask in relay_masks(t):
+                    source = flipped(me_z, mask + 1, nz)
+                    from_z(ag, k, ag_ss, ag_rs, source, t).wait_recv()
+                    image = image + forward(t, source)
         low, high = image[:half], image[half:]
         mine = jnp.where(core == 0, low, high)
         y_send[k] = jnp.where(core == 0, high, low).astype(jnp.bfloat16)
         y_copy(k).start()
+        for source in z_from:
+            from_z(nz_scalar, k, nz_ss, nz_rs, source).wait_recv()
         npar_scalar[k, me_p] = jnp.broadcast_to(z_row(nz_scalar, k), (8, LANES))
         for peer in p_peers:
             to_par(npar_scalar, k, np_ss, np_rs, peer).start()
@@ -410,8 +442,12 @@
         for peer in z_peers:
             for s in range(SUB):
                 rs_copy(k, peer, s).wait_send()
-                to_z(ag, k, ag_ss, ag_rs, peer, s).wait_send()
             to_z(nz_scalar, k, nz_ss, nz_rs, peer).wait_send()
+        for s in range(SUB):
+            for mask in sent_masks(s):
+                to_z(ag, k, ag_ss, ag_rs, flipped(me_z, mask, nz), s).wait_send()
+            for mask in relay_masks(s):
+                relay(k, flipped(me_z, mask, nz), s).wait_send()
         y_copy(k).wait_send()
         for copy in halo_copies(k):
             copy.wait_send()
@@ -424,6 +460,29 @@
     step = to_column(gg_ref[0:1] / curvature(ITERS), sets)
     apply_step(step)
     finish_scalars(ITERS)
+
+
+def finish_kernel(x_ref, r_ref, x_out, r_out, x_sem, r_sem):
+    copies = (
+        pltpu.make_async_copy(x_ref, x_out, x_sem),
+        pltpu.make_async_copy(r_ref, r_out, r_sem),
+    )
+    for copy in copies:
+        copy.start()
+    for copy in copies:
+        copy.wait()
+
+
+def finish(x, r):
+    vmem = pl.BlockSpec(memory_space=pltpu.VMEM)
+    space = pl.BlockSpec(memory_space=pl.ANY)
+    return pl.pallas_call(
+        finish_kernel,
+        out_shape=(jax.ShapeDtypeStruct(x.shape, x.dtype), jax.ShapeDtypeStruct(r.shape, r.dtype)),
+        in_specs=[vmem, vmem],
+        out_specs=(space, space),
+        scratch_shapes=[pltpu.SemaphoreType.DMA, pltpu.SemaphoreType.DMA],
+    )(x, r)
 
 
 def on_device_kernel(nz, npar, green_matrix, observed):
@@ -466,6 +525,7 @@
             dma((nz, SUB)),
             dma((n, nz, SUB)), dma((n, nz, SUB)),
             dma((n, nz, SUB)), dma((n, nz, SUB)),
+            dma((n, nz, SUB)),
             dma((n,)), dma((n,)),
             dma((n, npar)), dma((n, npar)),
             dma((n, 2)), dma((n, 2)),
@@ -488,7 +548,7 @@
         width = cells // (nz * SUB)
         fits = cells % (nz * SUB * GRID) == 0 and width >= 2 * GRID and nz & (nz - 1) == 0
         if fits and nz > 1 and npar % 2 == 0 and sets % 32 == 0 and sets <= LANES:
-            return on_device_kernel(nz, npar, green_matrix, observed)
+            return finish(*on_device_kernel(nz, npar, green_matrix, observed))
         return on_device(green_matrix, observed)
 
     return jax.shard_map(

time: 114 us -> 112 us (0.982)
  local copies, waits for them, and re-layouts: 3.45 us -> 0 us
    unnamed x2 -> x0, local copies, waits for them, and re-layouts: 3.45 us -> none
    pallas_call x0 -> x1, Pallas kernels: none -> 1.92 us  [finish(): pl.pallas_call(finish_kernel, out_shape=(jax.ShapeDtypeStruct(x.shape, x....]
where the time goes in v3:
time: 112 us
  Pallas kernels  111 us (99%)
    pallas_call x1, Pallas kernels, on_device_kernel(): pl.pallas_call(functools.partial(cgls_kernel, nz, npar), out_shape=(jax.S...  109 us

profile of v3, /device:TPU:0, one launch (start us, length us, event | category | flops | bytes accessed | tf_op | source)
XLA Modules:
  0.0 111.8 jit_solution(8964606571877475574)
XLA Ops:
  0.6 109.2 %shard_map.41 = (f32[32,4096]{1,0:T(8,128)}, f32[32,1152]{1,0:T(8,128)}) custom-call(bf16[1152,4096]{1,0:T(8,128)(2,1)} %green_hbm.1, bf16[32,1152]{1,0:T(8,128)(2,1)} %obs_ref.1), custom_call_target="tpu_custom_call" | custom-call | tf_op jit(solution)/shard_map/pallas_call | solution.py:497
  109.9 1.9 %shard_map.42 = (f32[32,4096]{1,0:T(8,128)}, f32[32,1152]{1,0:T(8,128)}) custom-call(f32[32,4096]{1,0:T(8,128)} %get-tuple-element.4.x_ref, f32[32,1152]{1,0:T(8,128)} %get-tuple-element.5.r_ref), custom_call_target="tpu_custom_call" | custom-call | tf_op jit(solution)/shard_map/pallas_call | solution.py:479

commit v4 on v3

--- a/solution.py
+++ b/solution.py
@@ -385,16 +385,15 @@
         for s in range(SUB):
             for mask in sent_masks(s)[::-1]:
                 source = flipped(me_z, mask, nz)
+                if s + 1 == SUB and mask == nz // 2:
+                    for t in range(SUB):
+                        for held in relay_masks(t):
+                            distant = flipped(me_z, held + 1, nz)
+                            from_z(ag, k, ag_ss, ag_rs, distant, t).wait_recv()
+                            image = image + forward(t, distant)
                 if mask not in relay_masks(s):
                     from_z(ag, k, ag_ss, ag_rs, source, s).wait_recv()
                 image = image + forward(s, source)
-            if s + 2 <= SUB:
-                continue
-            for t in range(SUB):
-                for mask in relay_masks(t):
-                    source = flipped(me_z, mask + 1, nz)
-                    from_z(ag, k, ag_ss, ag_rs, source, t).wait_recv()
-                    image = image + forward(t, source)
         low, high = image[:half], image[half:]
         mine = jnp.where(core == 0, low, high)
         y_send[k] = jnp.where(core == 0, high, low).astype(jnp.bfloat16)

time: 112 us -> 113 us (level)
  no operation moved by 1% of the time
where the time goes in v4:
time: 113 us; the launch traced here: 112 us
  Pallas kernels  112 us (99%)
    pallas_call x1, Pallas kernels, on_device_kernel(): pl.pallas_call(functools.partial(cgls_kernel, nz, npar), out_shape=(jax.S...  110 us

profile of v4, /device:TPU:0, one launch (start us, length us, event | category | flops | bytes accessed | tf_op | source)
XLA Modules:
  0.0 112.4 jit_solution(8020902365440295785)
XLA Ops:
  0.6 109.9 %shard_map.41 = (f32[32,4096]{1,0:T(8,128)}, f32[32,1152]{1,0:T(8,128)}) custom-call(bf16[1152,4096]{1,0:T(8,128)(2,1)} %green_hbm.1, bf16[32,1152]{1,0:T(8,128)(2,1)} %obs_ref.1), custom_call_target="tpu_custom_call" | custom-call | tf_op jit(solution)/shard_map/pallas_call | solution.py:496
  110.5 1.9 %shard_map.42 = (f32[32,4096]{1,0:T(8,128)}, f32[32,1152]{1,0:T(8,128)}) custom-call(f32[32,4096]{1,0:T(8,128)} %get-tuple-element.4.x_ref, f32[32,1152]{1,0:T(8,128)} %get-tuple-element.5.r_ref), custom_call_target="tpu_custom_call" | custom-call | tf_op jit(solution)/shard_map/pallas_call | solution.py:478
